TPU v7x, 128 devices: a whole 4x4x4 slice. The times are simulated.
128 devices in a mesh: row: 8 (over z, core), col: 16 (over y, x).
Axes of the slice: x: 4, y: 4, z: 4, core: 2. Of those that a mesh axis runs over, the one named last changes fastest.
Arguments:
- real_feats: bfloat16 [16384, 2048], P(('row', 'col')), may hold values from 0 to 8, as said below
- fake_feats: bfloat16 [16384, 2048], P(('row', 'col')), may hold values from 0 to 8, as said below
Outputs:
- proof_real: float32 [16384], P(('row', 'col'))
- proof_fake: float32 [16384], P(('row', 'col'))
- kid: float32 [], replicated
Inputs may be any that keep to these rules, and one draw needn't show every extreme that they name: `real_feats`: nonnegative features. `fake_feats`: nonnegative features.
All inputs are finite; a program needn't handle non-finite values.
Results may differ from a plain program's by a relative error of at most 0.0003.
Values may be sent and summed in bfloat16 or wider, within the bound.
No kernel may reach another device: no remote copies, remote signals or barrier semaphores. Data moves between devices by JAX's collectives and lax.ppermute only.
A program may use at most 128 MiB of HBM per device.

v0:
```python
import jax
import jax.numpy as jnp
from jax import lax
from jax.sharding import Mesh
from jax.sharding import PartitionSpec as P

ROW = ("row_0", "row_1")
COL = ("col_0", "col_1")
ROW_COL = ("row_0", "row_1", "col_0", "col_1")


def in_one_piece(arrays, axis, dim, along):
    both = jnp.concatenate(arrays, axis=along)
    out, at, finished = (lax.all_gather(both, axis, axis=dim, tiled=True), 0, [])
    for a in arrays:
        finished.append(lax.slice_in_dim(out, at, at + a.shape[along], axis=along))
        at += a.shape[along]
    return tuple(finished)


def split_up(value, dim, length):
    before, after = (value.shape[:dim], value.shape[dim + 1 :])
    return jnp.moveaxis(value.reshape(*before, length, -1, *after), dim, 0)


def sum_at_owner(value, axis, dim):
    length = lax.axis_size(axis)
    blocks = lax.all_to_all(split_up(value, dim, length), axis, 0, 0, tiled=True)
    return jnp.sum(blocks, axis=0)


def over_axes(value, axes):
    for axis in axes:
        value = lax.psum(value, axis)
    return value


def kernel_block(left, right, width):
    inner = lax.dot_general(
        left, right, (((1,), (1,)), ((), ())), preferred_element_type=jnp.float32
    )
    shifted = inner / width + 1.0
    return shifted * shifted * shifted


def shards(real_feats, fake_feats):
    rows_dev = real_feats.shape[0]
    width = real_feats.shape[1]
    n_row = lax.axis_size(ROW)
    n_col = lax.axis_size(COL)
    total = float(rows_dev * n_row * n_col)
    row_count = rows_dev * n_col
    col_count = rows_dev * n_row
    col_real, col_fake = (
        lax.all_gather(real_feats, ROW, axis=0, tiled=True),
        lax.all_gather(fake_feats, ROW, axis=0, tiled=True),
    )
    places = jnp.arange(col_count, dtype=jnp.int32)
    col_ids = places // rows_dev * row_count + lax.axis_index(COL) * rows_dev + places % rows_dev
    row_base = lax.axis_index(ROW) * row_count
    rows_real, rows_fake = in_one_piece((real_feats, fake_feats), COL, 0, 1)
    count = rows_real.shape[0]
    row_ids = row_base + jnp.arange(count, dtype=jnp.int32)
    off_diag = row_ids[:, None] != col_ids[None, :]
    same_real = jnp.where(off_diag, kernel_block(rows_real, col_real, width), 0.0)
    same_fake = jnp.where(off_diag, kernel_block(rows_fake, col_fake, width), 0.0)
    cross = kernel_block(rows_real, col_fake, width)
    first = jnp.sum(same_real, axis=1) / (total - 1.0) - jnp.sum(cross, axis=1) / total
    second = jnp.sum(same_fake, axis=1) / (total - 1.0)
    column = jnp.sum(cross, axis=0) / total
    first, second, column = (first, second, column)
    owned_first, owned_second = (sum_at_owner(first, COL, 0), sum_at_owner(second, COL, 0))
    owned_column = sum_at_owner(column, ROW, 0)
    proof_fake = owned_second - owned_column
    kid = over_axes(jnp.sum(owned_first) + jnp.sum(proof_fake), ROW_COL) / total
    return (owned_first, proof_fake, kid)


def solution(mesh):
    split = Mesh(mesh.devices.reshape(4, 2, 4, 4), ("row_0", "row_1", "col_0", "col_1"))
    placed = (P(ROW_COL, None), P(ROW_COL, None))
    return jax.shard_map(
        shards,
        mesh=split,
        in_specs=placed,
        out_specs=(P(ROW_COL), P(ROW_COL), P()),
        check_vma=False,
    )
```

profile of v0, /device:TPU:0, one launch (start us, length us, event | category | flops | bytes accessed | tf_op | source)
XLA Modules:
  0.0 272.9 jit_solution(2580525084667997164)
XLA Ops:
  7.2 0.7 all-gather.8.cloned.1.call-update
  7.9 2.4 pad_maximum_fusion
  10.3 0.0 all-gather.6.cloned.1.call-start
  10.4 0.7 all-gather.6.cloned.1.call-update
  11.1 33.4 %all-gather.8.cloned.1.call-done = bf16[1024,2048]{1,0:T(8,128)(2,1)} async-done(((bf16[128,2048]{1,0:T(8,128)(2,1)}), bf16[1024,2048]{1,0:T(8,128)(2,1)}) %all-gather.8.cloned.1.call-update) | async-done | bytes 4194320 | tf_op jit(solution)/shard_map/all_gather | solution.py:56
  44.5 113.0 %all-gather.4.cloned.1.call-done = bf16[2048,4096]{1,0:T(8,128)(2,1)} async-done(((bf16[128,4096]{1,0:T(8,128)(2,1)}), bf16[2048,4096]{1,0:T(8,128)(2,1)}) %all-gather.4.cloned.1.call-update) | async-done | bytes 16777232 | tf_op jit(solution)/shard_map/all_gather | solution.py:14
  157.5 13.0 %fusion.8 = (f32[1024]{0:T(1024)S(1)}, f32[2048]{0:T(1024)S(1)}) fusion(bf16[1024,2048]{1,0:T(8,128)(2,1)} %all-gather.8.cloned.1.call-done, bf16[2048,4096]{1,0:T(8,128)(2,1)} %all-gather.4.cloned.1.call-done), kind=kOutput, calls=%fused_computation.13 | convolution fusion | flops 8602514432 | bytes 12595200 | tf_op jit(solution)/shard_map/dot_general | solution.py:39
  170.5 0.6 broadcast_multiply_fusion.1
  171.1 4.4 %all-to-all-start.2 = ((f32[8,1,128]{2,1,0:T(1,128)}), f32[8,1,128]{2,1,0:T(1,128)S(1)}, u32[]{:S(2)}, u32[]{:S(2)}) async-start(f32[8,1,128]{2,1,0:T(1,128)} %bitcast.4), calls=%async_computation.2 | async-start | bytes 8192 | tf_op jit(solution)/shard_map/all_to_all | solution.py:28
  175.5 13.4 %fusion.1 = f32[2048]{0:T(1024)S(1)} fusion(bf16[1024,2048]{1,0:T(8,128)(2,1)} %all-gather.8.cloned.1.call-done, bf16[2048,4096]{1,0:T(8,128)(2,1)} %all-gather.4.cloned.1.call-done, s32[2048]{0:T(1024)S(1)} %iota_add_fusion, s32[1024]{0:T(1024)S(1)} %fusion.22), kind=kOutput, calls=%fused_computation.6 | convolution fusion | flops 8604612608 | bytes 12603392 | tf_op jit(solution)/shard_map/dot_general | solution.py:39
  189.0 2.3 all-gather.6.cloned.1.call-done
  191.3 13.3 %fusion = f32[2048]{0:T(1024)S(1)} fusion(bf16[1024,2048]{1,0:T(8,128)(2,1)} %all-gather.6.cloned.1.call-done, bf16[2048,4096]{1,0:T(8,128)(2,1)} %all-gather.4.cloned.1.call-done, s32[2048]{0:T(1024)S(1)} %iota_add_fusion, s32[1024]{0:T(1024)S(1)} %fusion.22), kind=kOutput, calls=%fused_computation.5 | convolution fusion | flops 8604612608 | bytes 12603392 | tf_op jit(solution)/shard_map/dot_general | solution.py:39
  204.6 0.6 broadcast_multiply_fusion
  205.2 6.8 %all-to-all-start.1 = ((f32[16,1,128]{2,1,0:T(1,128)}), f32[16,1,128]{2,1,0:T(1,128)S(1)}, u32[]{:S(2)}, u32[]{:S(2)}) async-start(f32[16,1,128]{2,1,0:T(1,128)} %bitcast.2), calls=%async_computation.1 | async-start | bytes 16384 | tf_op jit(solution)/shard_map/all_to_all | solution.py:28
  212.0 0.6 multiply_subtract_fusion
  212.6 6.8 %all-to-all-done.1 = f32[16,1,128]{2,1,0:T(1,128)S(1)} async-done(((f32[16,1,128]{2,1,0:T(1,128)}), f32[16,1,128]{2,1,0:T(1,128)S(1)}, u32[]{:S(2)}, u32[]{:S(2)}) %all-to-all-start.1) | async-done | bytes 8224 | tf_op jit(solution)/shard_map/all_to_all | solution.py:28
  219.4 3.4 %all-to-all-start = ((f32[16,1,128]{2,1,0:T(1,128)}), f32[16,1,128]{2,1,0:T(1,128)S(1)}, u32[]{:S(2)}, u32[]{:S(2)}) async-start(f32[16,1,128]{2,1,0:T(1,128)} %bitcast), calls=%async_computation | async-start | bytes 16384 | tf_op jit(solution)/shard_map/all_to_all | solution.py:28
  222.9 7.5 %all-to-all-done = f32[16,1,128]{2,1,0:T(1,128)S(1)} async-done(((f32[16,1,128]{2,1,0:T(1,128)}), f32[16,1,128]{2,1,0:T(1,128)S(1)}, u32[]{:S(2)}, u32[]{:S(2)}) %all-to-all-start) | async-done | bytes 8224 | tf_op jit(solution)/shard_map/all_to_all | solution.py:28
  230.4 0.6 fusion.24
  231.0 1.2 fusion.25
  233.5 9.0 %psum.28 = f32[]{:T(128)} all-reduce(f32[]{:T(128)S(6)} %add.79), channel_id=1, replica_groups=mesh['row_0'=4,'row_1'=2,'col_0'=4,'col_1'=4] {'row_0'}, use_global_device_ids=true, to_apply=%region_9.10 | all-reduce | flops 1 | bytes 8 | tf_op jit(solution)/shard_map/psum | solution.py:34
  242.5 3.1 %psum.29 = f32[]{:T(128)} all-reduce(f32[]{:T(128)} %psum.28), channel_id=1, replica_groups=mesh['row_0'=4,'row_1'=2,'col_0'=4,'col_1'=4] {'row_1'}, use_global_device_ids=true, to_apply=%region_10.11 | all-reduce | flops 1 | bytes 8 | tf_op jit(solution)/shard_map/psum | solution.py:34
  245.6 9.5 %psum.30 = f32[]{:T(128)} all-reduce(f32[]{:T(128)} %psum.29), channel_id=1, replica_groups=mesh['row_0'=4,'row_1'=2,'col_0'=4,'col_1'=4] {'col_0'}, use_global_device_ids=true, to_apply=%region_11.12 | all-reduce | flops 1 | bytes 8 | tf_op jit(solution)/shard_map/psum | solution.py:34
  255.1 9.5 %psum.31 = f32[]{:T(128)} all-reduce(f32[]{:T(128)} %psum.30), channel_id=1, replica_groups=mesh['row_0'=4,'row_1'=2,'col_0'=4,'col_1'=4] {'col_1'}, use_global_device_ids=true, to_apply=%region_12.13 | all-reduce | flops 1 | bytes 8 | tf_op jit(solution)/shard_map/psum | solution.py:34
  (8 shorter events, 0.1 us)
Async XLA Ops:
  7.2 37.3 %all-gather.8.cloned.1.call-start = ((), (), s32[]{:S(2)}) async-start(), calls=%async_computation.5 | async-start | bytes 4718592 | tf_op jit(solution)/shard_map/all_gather | solution.py:56
  7.9 149.6 %all-gather.4.cloned.1.call-start = ((), (), s32[]{:S(2)}) async-start(), calls=%async_computation.3 | async-start | bytes 17825792 | tf_op jit(solution)/shard_map/all_gather | solution.py:14
  10.3 181.0 %all-gather.6.cloned.1.call-start = ((), (), s32[]{:S(2)}) async-start(), calls=%async_computation.4 | async-start | bytes 4718592 | tf_op jit(solution)/shard_map/all_gather | solution.py:55
  171.1 34.1 %all-to-all-start.2 = ((f32[8,1,128]{2,1,0:T(1,128)}), f32[8,1,128]{2,1,0:T(1,128)S(1)}, u32[]{:S(2)}, u32[]{:S(2)}) async-start(f32[8,1,128]{2,1,0:T(1,128)} %bitcast.4), calls=%async_computation.2 | async-start | bytes 8192 | tf_op jit(solution)/shard_map/all_to_all | solution.py:28
  205.2 14.2 %all-to-all-start.1 = ((f32[16,1,128]{2,1,0:T(1,128)}), f32[16,1,128]{2,1,0:T(1,128)S(1)}, u32[]{:S(2)}, u32[]{:S(2)}) async-start(f32[16,1,128]{2,1,0:T(1,128)} %bitcast.2), calls=%async_computation.1 | async-start | bytes 16384 | tf_op jit(solution)/shard_map/all_to_all | solution.py:28
  219.4 10.9 %all-to-all-start = ((f32[16,1,128]{2,1,0:T(1,128)}), f32[16,1,128]{2,1,0:T(1,128)S(1)}, u32[]{:S(2)}, u32[]{:S(2)}) async-start(f32[16,1,128]{2,1,0:T(1,128)} %bitcast), calls=%async_computation | async-start | bytes 16384 | tf_op jit(solution)/shard_map/all_to_all | solution.py:28
Sparse Core Ops, SparseCore 0:
  9.7 34.7 all-gather.7
  46.6 110.8 all-gather.3
  159.2 32.0 all-gather.5
where the time goes:
time: 273 us
  waiting for transfers between devices  164 us (60%)
  matrix products  39.7 us (15%)
  blocking collectives  31.1 us (11%)
  between operations  16.9 us (6%)
  starting transfers between devices  14.7 us (5%)
  other arithmetic  5.99 us (2%)
    all_gather x1, waiting for transfers between devices, in_one_piece(): lax.all_gather(both, axis, axis=dim, tiled=True)  113 us
    dot_general x3, matrix products, kernel_block(): lax.dot_general(left, right, (((1,), (1,)), ((), ())), preferred_element_...  39.7 us
    all_gather x1, waiting for transfers between devices, shards(): lax.all_gather(fake_feats, ROW, axis=0, tiled=True)  33.4 us
    psum x4, blocking collectives, over_axes(): value = lax.psum(value, axis)  31.1 us
    all_to_all x3, starting transfers between devices, sum_at_owner(): lax.all_to_all(split_up(value, dim, length), axis, 0, 0, tiled=True)  14.6 us
    all_to_all x3, waiting for transfers between devices, sum_at_owner(): lax.all_to_all(split_up(value, dim, length), axis, 0, 0, tiled=True)  14.3 us
  transfers between devices with their start and end apart: 6, of which 5 were waited for; matrix products, arithmetic and copies ran while one was open for 16% of the time, Pallas kernels for 0%

commit v1 on v0

--- a/solution.py
+++ b/solution.py
@@ -53,7 +53,9 @@
     col_count = rows_dev * n_row
     col_real, col_fake = (
         lax.all_gather(real_feats, ROW, axis=0, tiled=True),
-        lax.all_gather(fake_feats, ROW, axis=0, tiled=True),
+        jnp.concatenate(
+            lax.all_to_all(jnp.stack([fake_feats] * lax.axis_size(ROW)), ROW, 0, 0), axis=0
+        ),
     )
     places = jnp.arange(col_count, dtype=jnp.int32)
     col_ids = places // rows_dev * row_count + lax.axis_index(COL) * rows_dev + places % rows_dev

time: 273 us -> 240 us (0.88)
  waiting for transfers between devices: 164 us -> 122 us
  starting transfers between devices: 14.7 us -> 20.1 us
  local copies, waits for them, and re-layouts: 0 us -> 3.55 us
    all_gather x1, waiting for transfers between devices: 113 us -> 55.4 us  [in_one_piece(): lax.all_gather(both, axis, axis=dim, tiled=True)]
    all_to_all x0 -> x1, waiting for transfers between devices: none -> 49 us  [shards(): lax.all_to_all(jnp.stack([fake_feats] * lax.axis_size(ROW)), ROW, 0, 0)]
    all_gather x1 -> x0, waiting for transfers between devices: 33.4 us -> none  [shards(): lax.all_gather(fake_feats, ROW, axis=0, tiled=True)]
    all_to_all x0 -> x1, starting transfers between devices: none -> 5.43 us  [shards(): lax.all_to_all(jnp.stack([fake_feats] * lax.axis_size(ROW)), ROW, 0, 0)]
    another operation x0 -> x1, local copies, waits for them, and re-layouts: none -> 3.55 us  [shards(): jnp.stack([fake_feats] * lax.axis_size(ROW))]
  transfers between devices with their start and end apart: 6 -> 6, of which waited for: 5 -> 5; matrix products, arithmetic and copies ran while one was open for 16% -> 19% of each run, Pallas kernels for 0% -> 0%
where the time goes in v1:
time: 240 us; the launch traced here: 239 us
  waiting for transfers between devices  122 us (51%)
  matrix products  39.7 us (17%)
  blocking collectives  31.1 us (13%)
  starting transfers between devices  20.1 us (8%)
  between operations  17.2 us (7%)
  other arithmetic  5.97 us (2%)
  local copies, waits for them, and re-layouts  3.55 us (1%)
    all_gather x1, waiting for transfers between devices, in_one_piece(): lax.all_gather(both, axis, axis=dim, tiled=True)  55.4 us
    all_to_all x1, waiting for transfers between devices, shards(): lax.all_to_all(jnp.stack([fake_feats] * lax.axis_size(ROW)), ROW, 0, 0)  49 us
    dot_general x3, matrix products, kernel_block(): lax.dot_general(left, right, (((1,), (1,)), ((), ())), preferred_element_...  39.7 us
    psum x4, blocking collectives, over_axes(): value = lax.psum(value, axis)  31.1 us
    all_to_all x3, starting transfers between devices, sum_at_owner(): lax.all_to_all(split_up(value, dim, length), axis, 0, 0, tiled=True)  14.6 us
    all_to_all x3, waiting for transfers between devices, sum_at_owner(): lax.all_to_all(split_up(value, dim, length), axis, 0, 0, tiled=True)  14.3 us
    all_to_all x1, starting transfers between devices, shards(): lax.all_to_all(jnp.stack([fake_feats] * lax.axis_size(ROW)), ROW, 0, 0)  5.43 us
  transfers between devices with their start and end apart: 6, of which 5 were waited for; matrix products, arithmetic and copies ran while one was open for 19% of the time, Pallas kernels for 0%

profile of v1, /device:TPU:0, one launch (start us, length us, event | category | flops | bytes accessed | tf_op | source)
XLA Modules:
  0.0 239.4 jit_solution(3388679062071986)
XLA Ops:
  7.2 2.3 pad_maximum_fusion
  9.6 3.5 %stack.2 = bf16[8,128,2048]{2,1,0:T(8,128)(2,1)} broadcast(bf16[128,2048]{1,0:T(8,128)(2,1)} %param.3), dimensions={1,2} | broadcast | bytes 4718592 | tf_op jit(solution)/shard_map/stack | solution.py:57
  13.1 5.4 %all-to-all-start = ((bf16[8,128,2048]{2,1,0:T(8,128)(2,1)}), bf16[8,128,2048]{2,1,0:T(8,128)(2,1)}, u32[]{:S(2)}, u32[]{:S(2)}) async-start(bf16[8,128,2048]{2,1,0:T(8,128)(2,1)} %stack.2), calls=%async_computation | async-start | bytes 8388608 | tf_op jit(solution)/shard_map/all_to_all | solution.py:57
  18.6 0.7 all-gather.5.cloned.1.call-update
  19.3 49.0 %all-to-all-done = bf16[8,128,2048]{2,1,0:T(8,128)(2,1)} async-done(((bf16[8,128,2048]{2,1,0:T(8,128)(2,1)}), bf16[8,128,2048]{2,1,0:T(8,128)(2,1)}, u32[]{:S(2)}, u32[]{:S(2)}) %all-to-all-start) | async-done | bytes 4194336 | tf_op jit(solution)/shard_map/all_to_all | solution.py:57
  68.3 55.4 %all-gather.3.cloned.1.call-done = bf16[2048,4096]{1,0:T(8,128)(2,1)} async-done(((bf16[128,4096]{1,0:T(8,128)(2,1)}), bf16[2048,4096]{1,0:T(8,128)(2,1)}) %all-gather.3.cloned.1.call-update) | async-done | bytes 16777232 | tf_op jit(solution)/shard_map/all_gather | solution.py:14
  123.7 13.0 %fusion.8 = (f32[1024]{0:T(1024)S(1)}, f32[2048]{0:T(1024)S(1)}) fusion(bf16[1024,2048]{1,0:T(8,128)(2,1)} %bitcast, bf16[2048,4096]{1,0:T(8,128)(2,1)} %all-gather.3.cloned.1.call-done), kind=kOutput, calls=%fused_computation.13 | convolution fusion | flops 8602514432 | bytes 12595200 | tf_op jit(solution)/shard_map/dot_general | solution.py:39
  136.7 0.6 broadcast_multiply_fusion.1
  137.3 4.4 %all-to-all-start.3 = ((f32[8,1,128]{2,1,0:T(1,128)}), f32[8,1,128]{2,1,0:T(1,128)S(1)}, u32[]{:S(2)}, u32[]{:S(2)}) async-start(f32[8,1,128]{2,1,0:T(1,128)} %bitcast.5), calls=%async_computation.3 | async-start | bytes 8192 | tf_op jit(solution)/shard_map/all_to_all | solution.py:28
  141.7 13.4 %fusion.1 = f32[2048]{0:T(1024)S(1)} fusion(bf16[1024,2048]{1,0:T(8,128)(2,1)} %bitcast, bf16[2048,4096]{1,0:T(8,128)(2,1)} %all-gather.3.cloned.1.call-done, s32[2048]{0:T(1024)S(1)} %iota_add_fusion, s32[1024]{0:T(1024)S(1)} %fusion.22), kind=kOutput, calls=%fused_computation.6 | convolution fusion | flops 8604612608 | bytes 12603392 | tf_op jit(solution)/shard_map/dot_general | solution.py:39
  155.2 2.3 all-gather.5.cloned.1.call-done
  157.5 13.3 %fusion = f32[2048]{0:T(1024)S(1)} fusion(bf16[1024,2048]{1,0:T(8,128)(2,1)} %all-gather.5.cloned.1.call-done, bf16[2048,4096]{1,0:T(8,128)(2,1)} %all-gather.3.cloned.1.call-done, s32[2048]{0:T(1024)S(1)} %iota_add_fusion, s32[1024]{0:T(1024)S(1)} %fusion.22), kind=kOutput, calls=%fused_computation.5 | convolution fusion | flops 8604612608 | bytes 12603392 | tf_op jit(solution)/shard_map/dot_general | solution.py:39
  170.8 0.6 broadcast_multiply_fusion
  171.4 6.8 %all-to-all-start.2 = ((f32[16,1,128]{2,1,0:T(1,128)}), f32[16,1,128]{2,1,0:T(1,128)S(1)}, u32[]{:S(2)}, u32[]{:S(2)}) async-start(f32[16,1,128]{2,1,0:T(1,128)} %bitcast.3), calls=%async_computation.2 | async-start | bytes 16384 | tf_op jit(solution)/shard_map/all_to_all | solution.py:28
  178.2 0.6 multiply_subtract_fusion
  178.8 6.8 %all-to-all-done.2 = f32[16,1,128]{2,1,0:T(1,128)S(1)} async-done(((f32[16,1,128]{2,1,0:T(1,128)}), f32[16,1,128]{2,1,0:T(1,128)S(1)}, u32[]{:S(2)}, u32[]{:S(2)}) %all-to-all-start.2) | async-done | bytes 8224 | tf_op jit(solution)/shard_map/all_to_all | solution.py:28
  185.6 3.4 %all-to-all-start.1 = ((f32[16,1,128]{2,1,0:T(1,128)}), f32[16,1,128]{2,1,0:T(1,128)S(1)}, u32[]{:S(2)}, u32[]{:S(2)}) async-start(f32[16,1,128]{2,1,0:T(1,128)} %bitcast.1), calls=%async_computation.1 | async-start | bytes 16384 | tf_op jit(solution)/shard_map/all_to_all | solution.py:28
  189.1 7.5 %all-to-all-done.1 = f32[16,1,128]{2,1,0:T(1,128)S(1)} async-done(((f32[16,1,128]{2,1,0:T(1,128)}), f32[16,1,128]{2,1,0:T(1,128)S(1)}, u32[]{:S(2)}, u32[]{:S(2)}) %all-to-all-start.1) | async-done | bytes 8224 | tf_op jit(solution)/shard_map/all_to_all | solution.py:28
  196.5 0.6 fusion.24
  197.1 1.2 fusion.25
  199.7 9.0 %psum.28 = f32[]{:T(128)} all-reduce(f32[]{:T(128)S(6)} %add.79), channel_id=1, replica_groups=mesh['row_0'=4,'row_1'=2,'col_0'=4,'col_1'=4] {'row_0'}, use_global_device_ids=true, to_apply=%region_9.10 | all-reduce | flops 1 | bytes 8 | tf_op jit(solution)/shard_map/psum | solution.py:34
  208.7 3.1 %psum.29 = f32[]{:T(128)} all-reduce(f32[]{:T(128)} %psum.28), channel_id=1, replica_groups=mesh['row_0'=4,'row_1'=2,'col_0'=4,'col_1'=4] {'row_1'}, use_global_device_ids=true, to_apply=%region_10.11 | all-reduce | flops 1 | bytes 8 | tf_op jit(solution)/shard_map/psum | solution.py:34
  211.8 9.5 %psum.30 = f32[]{:T(128)} all-reduce(f32[]{:T(128)} %psum.29), channel_id=1, replica_groups=mesh['row_0'=4,'row_1'=2,'col_0'=4,'col_1'=4] {'col_0'}, use_global_device_ids=true, to_apply=%region_11.12 | all-reduce | flops 1 | bytes 8 | tf_op jit(solution)/shard_map/psum | solution.py:34
  221.2 9.5 %psum.31 = f32[]{:T(128)} all-reduce(f32[]{:T(128)} %psum.30), channel_id=1, replica_groups=mesh['row_0'=4,'row_1'=2,'col_0'=4,'col_1'=4] {'col_1'}, use_global_device_ids=true, to_apply=%region_12.13 | all-reduce | flops 1 | bytes 8 | tf_op jit(solution)/shard_map/psum | solution.py:34
  (8 shorter events, 0.1 us)
Async XLA Ops:
  7.2 116.5 %all-gather.3.cloned.1.call-start = ((), (), s32[]{:S(2)}) async-start(), calls=%async_computation.4 | async-start | bytes 17825792 | tf_op jit(solution)/shard_map/all_gather | solution.py:14
  13.1 55.2 %all-to-all-start = ((bf16[8,128,2048]{2,1,0:T(8,128)(2,1)}), bf16[8,128,2048]{2,1,0:T(8,128)(2,1)}, u32[]{:S(2)}, u32[]{:S(2)}) async-start(bf16[8,128,2048]{2,1,0:T(8,128)(2,1)} %stack.2), calls=%async_computation | async-start | bytes 8388608 | tf_op jit(solution)/shard_map/all_to_all | solution.py:57
  18.5 138.9 %all-gather.5.cloned.1.call-start = ((), (), s32[]{:S(2)}) async-start(), calls=%async_computation.5 | async-start | bytes 4718592 | tf_op jit(solution)/shard_map/all_gather | solution.py:55
  137.3 34.1 %all-to-all-start.3 = ((f32[8,1,128]{2,1,0:T(1,128)}), f32[8,1,128]{2,1,0:T(1,128)S(1)}, u32[]{:S(2)}, u32[]{:S(2)}) async-start(f32[8,1,128]{2,1,0:T(1,128)} %bitcast.5), calls=%async_computation.3 | async-start | bytes 8192 | tf_op jit(solution)/shard_map/all_to_all | solution.py:28
  171.4 14.2 %all-to-all-start.2 = ((f32[16,1,128]{2,1,0:T(1,128)}), f32[16,1,128]{2,1,0:T(1,128)S(1)}, u32[]{:S(2)}, u32[]{:S(2)}) async-start(f32[16,1,128]{2,1,0:T(1,128)} %bitcast.3), calls=%async_computation.2 | async-start | bytes 16384 | tf_op jit(solution)/shard_map/all_to_all | solution.py:28
  185.6 10.9 %all-to-all-start.1 = ((f32[16,1,128]{2,1,0:T(1,128)}), f32[16,1,128]{2,1,0:T(1,128)S(1)}, u32[]{:S(2)}, u32[]{:S(2)}) async-start(f32[16,1,128]{2,1,0:T(1,128)} %bitcast.1), calls=%async_computation.1 | async-start | bytes 16384 | tf_op jit(solution)/shard_map/all_to_all | solution.py:28
Sparse Core Ops, SparseCore 0:
  10.1 113.5 all-gather.2
  125.4 32.0 all-gather.4
